TPU v7x, 32 devices: a 4x4x1 block of a 4x4x8 slice. The times are simulated.
32 devices in a mesh: replica: 1 (over z), dp: 32 (over y, x, core).
Axes of the slice: x: 4, y: 4, z: 1, core: 2. Of those that a mesh axis runs over, the one named last changes fastest.
The devices are a block of a 4x4x8 slice.
Arguments:
- x: bfloat16 [1024, 256], P(('replica', 'dp'))
- lengths: int32 [1024], P(('replica', 'dp'))
- cache: bfloat16 [2, 1024, 512, 576], P(None, ('replica', 'dp'))
- w_q: bfloat16 [2, 256, 1152], replicated
- w_o: bfloat16 [2, 1024, 256], replicated
- expert_ids: int32 [2, 1024, 6], P(None, ('replica', 'dp'))
- slots: int32 [2, 1024, 6], P(None, ('replica', 'dp'))
- route_w: float32 [2, 1024, 6], P(None, ('replica', 'dp'))
- w1_exp: bfloat16 [2, 64, 256, 176], P(None, 'dp')
- w3_exp: bfloat16 [2, 64, 256, 176], P(None, 'dp')
- w2_exp: bfloat16 [2, 64, 176, 256], P(None, 'dp')
- w1_sh: bfloat16 [2, 256, 352], P(None, None, 'dp')
- w3_sh: bfloat16 [2, 256, 352], P(None, None, 'dp')
- w2_sh: bfloat16 [2, 352, 256], P(None, 'dp')
Outputs:
- output: bfloat16 [1024, 256], P(('replica', 'dp'))
All inputs are finite; a program needn't handle non-finite values.
Results may differ from a plain program's by a relative error of at most 0.02.
Values are sent between devices in bfloat16 or wider.
A program may use at most 768 MiB of HBM per device.

v0:
```python
import jax
import jax.numpy as jnp
from jax import lax
from jax.sharding import PartitionSpec as P

NORM_EPS = 1e-6
ATT_SCALE = 1.0 / (192.0 ** 0.5)
LATENT = 512


def rms_norm(values):
    vals32 = values.astype(jnp.float32)
    return vals32 * lax.rsqrt(jnp.mean(vals32 * vals32, axis=-1, keepdims=True) + NORM_EPS)


def gated_hidden(tok_in, w_up, w_gate):
    gate_in = jnp.dot(tok_in, w_gate, preferred_element_type=jnp.float32)
    up_in = jnp.dot(tok_in, w_up, preferred_element_type=jnp.float32)
    return (jax.nn.silu(gate_in) * up_in).astype(jnp.bfloat16)


def local_attention(resid, lengths, cache_l, w_q_l, w_o_l):
    tok_count = resid.shape[0]
    seq_len, kv_dim = cache_l.shape[1], cache_l.shape[2]
    num_heads = w_q_l.shape[1] // kv_dim
    normed = rms_norm(resid).astype(jnp.bfloat16)
    queries = jnp.dot(normed, w_q_l, preferred_element_type=jnp.float32).astype(jnp.bfloat16)
    queries = queries.reshape(tok_count, num_heads, kv_dim)
    scores = jnp.einsum('bhc,btc->bht', queries, cache_l, preferred_element_type=jnp.float32) * ATT_SCALE
    valid = jnp.arange(seq_len)[None, None, :] < lengths[:, None, None]
    probs = jax.nn.softmax(jnp.where(valid, scores, -jnp.inf), axis=-1).astype(jnp.bfloat16)
    attn = jnp.einsum('bht,btc->bhc', probs, cache_l[:, :, :LATENT], preferred_element_type=jnp.float32)
    attn = attn.astype(jnp.bfloat16).reshape(tok_count, num_heads * LATENT)
    return (resid.astype(jnp.float32) + jnp.dot(attn, w_o_l, preferred_element_type=jnp.float32)).astype(jnp.bfloat16)


def route_select(ids_l, slot_l, experts, capacity):
    buf_rows = jnp.where(slot_l >= 0, ids_l * capacity + slot_l, -1)
    return (buf_rows[:, :, None] == jnp.arange(experts * capacity)).astype(jnp.bfloat16)


def solution(mesh):
    group = mesh.shape['dp']
    tok_axes = ('replica', 'dp')
    in_specs = (
        P(tok_axes, None), P(tok_axes), P(None, tok_axes, None, None),
        P(None, None, None), P(None, None, None),
        P(None, tok_axes, None), P(None, tok_axes, None), P(None, tok_axes, None),
        P(None, 'dp', None, None), P(None, 'dp', None, None), P(None, 'dp', None, None),
        P(None, None, 'dp'), P(None, None, 'dp'), P(None, 'dp', None),
    )

    def device_step(x, lengths, cache, w_q, w_o, expert_ids, slots, route_w, w1_exp, w3_exp, w2_exp, w1_sh, w3_sh, w2_sh):
        batch_dev, d_model = x.shape
        local_experts = w1_exp.shape[1]
        experts = local_experts * group
        top_k = expert_ids.shape[2]
        capacity = max(1, (2 * batch_dev * top_k) // experts)
        resid = x
        for layer_idx in range(cache.shape[0]):
            resid = local_attention(resid, lengths, cache[layer_idx], w_q[layer_idx], w_o[layer_idx])
            ffn_in = rms_norm(resid).astype(jnp.bfloat16)
            gathered = lax.all_gather(ffn_in, 'dp', axis=0, tiled=True)
            shared_h = gated_hidden(gathered, w1_sh[layer_idx], w3_sh[layer_idx])
            shared_part = jnp.dot(shared_h, w2_sh[layer_idx], preferred_element_type=jnp.float32)
            shared_out = lax.psum_scatter(shared_part, 'dp', scatter_dimension=0, tiled=True)
            select = route_select(expert_ids[layer_idx], slots[layer_idx], experts, capacity)
            dispatch = jnp.sum(select, axis=1)
            send_buf = jnp.einsum('br,bd->rd', dispatch, ffn_in, preferred_element_type=jnp.float32).astype(jnp.bfloat16)
            send_buf = send_buf.reshape(group, local_experts, capacity, d_model)
            recv_buf = lax.all_to_all(send_buf, 'dp', 0, 0, tiled=True)
            gate_in = jnp.einsum('sncd,ndf->nscf', recv_buf, w3_exp[layer_idx], preferred_element_type=jnp.float32)
            up_in = jnp.einsum('sncd,ndf->nscf', recv_buf, w1_exp[layer_idx], preferred_element_type=jnp.float32)
            hidden = (jax.nn.silu(gate_in) * up_in).astype(jnp.bfloat16)
            expert_out = jnp.einsum('nscf,nfd->sncd', hidden, w2_exp[layer_idx], preferred_element_type=jnp.float32).astype(jnp.bfloat16)
            returned = lax.all_to_all(expert_out, 'dp', 0, 0, tiled=True)
            returned = returned.reshape(experts * capacity, d_model)
            picked = jnp.einsum('cls,se->cle', select, returned, preferred_element_type=jnp.float32)
            routed = jnp.sum(route_w[layer_idx][:, :, None] * picked, axis=1)
            resid = (resid.astype(jnp.float32) + routed + shared_out).astype(jnp.bfloat16)
        return resid

    return jax.shard_map(device_step, mesh=mesh, in_specs=in_specs, out_specs=P(tok_axes, None), check_vma=False)
```

profile of v0, /device:TPU:97, one launch (start us, length us, event | category | flops | bytes accessed | tf_op | source)
XLA Modules:
  0.0 293.7 jit_solution(7096934623553952140)
XLA Ops:
  7.3 0.8 fusion.94
  8.1 1.3 convolution_convert_fusion.1
  9.6 25.4 %slice_bitcast_fusion.1 = (bf16[32,512,576]{1,2,0:T(8,128)(2,1)}, bf16[32,512,576]{1,2,0:T(8,128)(2,1)}) fusion(bf16[2,32,512,576]{2,3,1,0:T(8,128)(2,1)} %param.16), kind=kLoop, calls=%fused_computation.3 | loop fusion | bytes 75497472 | tf_op jit(solution)/shard_map/squeeze | solution.py:61
  35.1 9.2 %fusion.120 = (f32[32,2]{1,0:T(8,128)S(1)}, f32[32,2,512]{2,1,0:T(2,128)S(1)}) fusion(bf16[32,2,576]{2,1,0:T(2,128)(2,1)S(1)} %reshape.127, pred[32,512]{1,0:T(8,128)(4,1)S(1)} %iota_compare_fusion.4, bf16[2,32,512,576]{2,3,1,0:T(8,128)(2,1)} %param.16), kind=kOutput, calls=%fused_computation.159 | convolution fusion | flops 37880320 | bytes 19095808 | tf_op jit(solution)/shard_map/sub | solution.py:31
  44.4 8.2 %fusion.18 = bf16[32,2,512]{2,1,0:T(2,128)(2,1)S(1)} fusion(bf16[32,512,576]{1,2,0:T(8,128)(2,1)} %get-tuple-element.7, f32[32,2,512]{2,1,0:T(2,128)S(1)} %get-tuple-element.22, f32[32,2]{1,0:T(8,128)S(1)} %get-tuple-element.21), kind=kOutput, calls=%fused_computation.32 | convolution fusion | flops 33652736 | bytes 16974080 | tf_op jit(solution)/shard_map/bht,btc->bhc/dot_general | solution.py:32
  53.0 32.6 %all_gather.6 = bf16[1024,256]{1,0:T(8,128)(2,1)S(1)} all-gather(bf16[32,256]{1,0:T(8,128)(2,1)S(1)} %multiply_convert_fusion.1), channel_id=1, replica_groups=mesh['replica'=1,'dp'=32] {'dp'}, dimensions={0}, use_global_device_ids=true | all-gather | bytes 540672 | tf_op jit(solution)/shard_map/all_gather | solution.py:63
  87.1 1.6 fusion.27
  89.4 17.5 %all_to_all.20 = bf16[32,2,6,256]{3,1,2,0:T(2,128)(2,1)S(1)} all-to-all(bf16[32,2,6,256]{3,1,2,0:T(2,128)(2,1)S(1)} %copy.61), channel_id=1, replica_groups=mesh['replica'=1,'dp'=32] {'dp'}, dimensions={0} | all-to-all | bytes 393216 | tf_op jit(solution)/shard_map/all_to_all | solution.py:71
  107.1 1.4 fusion.8
  108.5 0.9 copy.64
  109.4 2.9 all-to-all-start.1
  112.5 7.8 %all-to-all-done.1 = bf16[32,2,6,256]{3,1,2,0:T(2,128)(2,1)S(1)} async-done(((bf16[32,2,6,256]{3,1,2,0:T(2,128)(2,1)}), bf16[32,2,6,256]{3,1,2,0:T(2,128)(2,1)S(1)}, u32[]{:S(2)}, u32[]{:S(2)}) %all-to-all-start.1) | async-done | bytes 196640 | tf_op jit(solution)/shard_map/all_to_all | solution.py:76
  120.7 41.0 %reduce-scatter.3.cloned.1.call-done = f32[32,256]{1,0:T(8,128)} async-done(((f32[1024,256]{1,0:T(8,128)}), f32[32,256]{1,0:T(8,128)}) %reduce-scatter.3.cloned.1.call-update) | async-done | bytes 32784 | tf_op jit(solution)/shard_map/reduce_scatter | solution.py:66
  161.7 0.9 fusion.96
  163.1 9.2 %fusion.121 = (f32[32,2]{1,0:T(8,128)S(1)}, f32[32,2,512]{2,1,0:T(2,128)S(1)}) fusion(bf16[32,2,576]{2,1,0:T(2,128)(2,1)S(1)} %reshape.131, pred[32,512]{1,0:T(8,128)(4,1)S(1)} %iota_compare_fusion.4, bf16[2,32,512,576]{2,3,1,0:T(8,128)(2,1)} %param.16), kind=kOutput, calls=%fused_computation.160 | convolution fusion | flops 37880320 | bytes 19095808 | tf_op jit(solution)/shard_map/sub | solution.py:31
  172.3 8.1 %fusion.21 = bf16[32,2,512]{2,1,0:T(2,128)(2,1)S(1)} fusion(bf16[32,512,576]{1,2,0:T(8,128)(2,1)} %get-tuple-element.8, f32[32,2,512]{2,1,0:T(2,128)S(1)} %get-tuple-element.26, f32[32,2]{1,0:T(8,128)S(1)} %get-tuple-element.25), kind=kOutput, calls=%fused_computation.33 | convolution fusion | flops 33652736 | bytes 16974080 | tf_op jit(solution)/shard_map/bht,btc->bhc/dot_general | solution.py:32
  180.8 29.7 %all_gather.7 = bf16[1024,256]{1,0:T(8,128)(2,1)S(1)} all-gather(bf16[32,256]{1,0:T(8,128)(2,1)S(1)} %multiply_convert_fusion), channel_id=1, replica_groups=mesh['replica'=1,'dp'=32] {'dp'}, dimensions={0}, use_global_device_ids=true | all-gather | bytes 540672 | tf_op jit(solution)/shard_map/all_gather | solution.py:63
  210.8 1.6 fusion.26
  213.0 17.6 %all_to_all.21 = bf16[32,2,6,256]{3,1,2,0:T(2,128)(2,1)S(1)} all-to-all(bf16[32,2,6,256]{3,1,2,0:T(2,128)(2,1)S(1)} %copy.73), channel_id=1, replica_groups=mesh['replica'=1,'dp'=32] {'dp'}, dimensions={0} | all-to-all | bytes 393216 | tf_op jit(solution)/shard_map/all_to_all | solution.py:71
  231.2 0.9 copy.76
  232.1 2.9 all-to-all-start.3
  235.0 8.1 %all-to-all-done.3 = bf16[32,2,6,256]{3,1,2,0:T(2,128)(2,1)S(1)} async-done(((bf16[32,2,6,256]{3,1,2,0:T(2,128)(2,1)}), bf16[32,2,6,256]{3,1,2,0:T(2,128)(2,1)S(1)}, u32[]{:S(2)}, u32[]{:S(2)}) %all-to-all-start.3) | async-done | bytes 196640 | tf_op jit(solution)/shard_map/all_to_all | solution.py:76
  243.4 42.0 %reduce-scatter.5.cloned.1.call-done = f32[32,256]{1,0:T(8,128)} async-done(((f32[1024,256]{1,0:T(8,128)}), f32[32,256]{1,0:T(8,128)}) %reduce-scatter.5.cloned.1.call-update) | async-done | bytes 32784 | tf_op jit(solution)/shard_map/reduce_scatter | solution.py:66
  285.4 1.4 add_convert_fusion
  (74 shorter events, 6.9 us)
Async XLA Ops:
  6.5 155.2 %reduce-scatter.3.cloned.1.call-start = ((), (), s32[]{:S(2)}) async-start(), calls=%async_computation.6 | async-start | bytes 1081344 | tf_op jit(solution)/shard_map/reduce_scatter | solution.py:66
  35.0 17.6 %copy-start.1 = (bf16[2,1024,256]{2,1,0:T(8,128)(2,1)S(1)}, bf16[2,1024,256]{2,1,0:T(8,128)(2,1)}, u32[]{:S(2)}) copy-start(bf16[2,1024,256]{2,1,0:T(8,128)(2,1)} %param.18) | copy-start | bytes 3145732
  35.0 17.6 %copy-start.3 = (bf16[32,256]{1,0:T(8,128)(2,1)S(1)}, bf16[32,256]{1,0:T(8,128)(2,1)}, u32[]{:S(2)}) copy-start(bf16[32,256]{1,0:T(8,128)(2,1)} %param.14) | copy-start | bytes 49156
  35.1 50.6 %copy-start.4 = (bf16[2,256,11]{1,0,2:T(2,128)(2,1)S(1)}, bf16[2,256,11]{1,0,2:T(2,128)(2,1)}, u32[]{:S(2)}) copy-start(bf16[2,256,11]{1,0,2:T(2,128)(2,1)} %param.26) | copy-start | bytes 33796
  35.1 51.2 %copy-start.5 = (bf16[2,256,11]{1,0,2:T(2,128)(2,1)S(1)}, bf16[2,256,11]{1,0,2:T(2,128)(2,1)}, u32[]{:S(2)}) copy-start(bf16[2,256,11]{1,0,2:T(2,128)(2,1)} %param.25) | copy-start | bytes 33796
  35.1 51.2 %copy-start.6 = (bf16[2,11,256]{2,0,1:T(2,128)(2,1)S(1)}, bf16[2,11,256]{2,0,1:T(2,128)(2,1)}, u32[]{:S(2)}) copy-start(bf16[2,11,256]{2,0,1:T(2,128)(2,1)} %param.27) | copy-start | bytes 33796
  35.1 53.7 %copy-start.10 = (s32[2,32,6]{1,0,2:T(2,128)S(1)}, s32[2,32,6]{1,0,2:T(2,128)}, u32[]{:S(2)}) copy-start(s32[2,32,6]{1,0,2:T(2,128)} %param.19) | copy-start | bytes 4612
  35.1 53.7 %copy-start.11 = (s32[2,32,6]{1,0,2:T(2,128)S(1)}, s32[2,32,6]{1,0,2:T(2,128)}, u32[]{:S(2)}) copy-start(s32[2,32,6]{1,0,2:T(2,128)} %param.20) | copy-start | bytes 4612
  35.1 71.8 %copy-start.2 = (bf16[2,2,256,176]{2,3,1,0:T(8,128)(2,1)S(1)}, bf16[2,2,256,176]{2,3,1,0:T(8,128)(2,1)}, u32[]{:S(2)}) copy-start(bf16[2,2,256,176]{2,3,1,0:T(8,128)(2,1)} %param.23) | copy-start | bytes 1081348
  44.3 68.2 %copy-start.9 = (f32[2,32,6]{1,0,2:T(2,128)S(1)}, f32[2,32,6]{1,0,2:T(2,128)}, u32[]{:S(2)}) copy-start(f32[2,32,6]{1,0,2:T(2,128)} %param.21) | copy-start | bytes 4612
  44.3 118.3 %copy-start = (bf16[2,256,1152]{2,1,0:T(8,128)(2,1)S(1)}, bf16[2,256,1152]{2,1,0:T(8,128)(2,1)}, u32[]{:S(2)}) copy-start(bf16[2,256,1152]{2,1,0:T(8,128)(2,1)} %param.17) | copy-start | bytes 3538948
  109.4 10.9 %all-to-all-start.1 = ((bf16[32,2,6,256]{3,1,2,0:T(2,128)(2,1)}), bf16[32,2,6,256]{3,1,2,0:T(2,128)(2,1)S(1)}, u32[]{:S(2)}, u32[]{:S(2)}) async-start(bf16[32,2,6,256]{3,1,2,0:T(2,128)(2,1)} %copy.64), calls=%async_computation.1 | async-start | bytes 393216 | tf_op jit(solution)/shard_map/all_to_all | solution.py:76
  112.3 173.2 %reduce-scatter.5.cloned.1.call-start = ((), (), s32[]{:S(2)}) async-start(), calls=%async_computation.7 | async-start | bytes 1081344 | tf_op jit(solution)/shard_map/reduce_scatter | solution.py:66
  163.0 47.5 %copy-start.7 = (bf16[1,256,11]{1,0,2:T(2,128)(2,1)S(1)}, bf16[1,256,11]{1,0,2:T(2,128)(2,1)}, u32[]{:S(2)}) copy-start(bf16[1,256,11]{1,0,2:T(2,128)(2,1)} %get-tuple-element.13) | copy-start | bytes 16900
  163.0 47.8 %copy-start.8 = (bf16[1,11,256]{2,0,1:T(2,128)(2,1)S(1)}, bf16[1,11,256]{2,0,1:T(2,128)(2,1)}, u32[]{:S(2)}) copy-start(bf16[1,11,256]{2,0,1:T(2,128)(2,1)} %get-tuple-element.11) | copy-start | bytes 16900
  163.0 67.8 %copy-start.12 = (bf16[2,2,176,256]{3,2,1,0:T(8,128)(2,1)S(1)}, bf16[2,2,176,256]{3,2,1,0:T(8,128)(2,1)}, u32[]{:S(2)}) copy-start(bf16[2,2,176,256]{3,2,1,0:T(8,128)(2,1)} %param.24) | copy-start | bytes 1081348
  163.1 67.8 %copy-start.13 = (bf16[2,2,256,176]{2,3,1,0:T(8,128)(2,1)S(1)}, bf16[2,2,256,176]{2,3,1,0:T(8,128)(2,1)}, u32[]{:S(2)}) copy-start(bf16[2,2,256,176]{2,3,1,0:T(8,128)(2,1)} %param.22) | copy-start | bytes 1081348
  232.1 11.0 %all-to-all-start.3 = ((bf16[32,2,6,256]{3,1,2,0:T(2,128)(2,1)}), bf16[32,2,6,256]{3,1,2,0:T(2,128)(2,1)S(1)}, u32[]{:S(2)}, u32[]{:S(2)}) async-start(bf16[32,2,6,256]{3,1,2,0:T(2,128)(2,1)} %copy.76), calls=%async_computation.4 | async-start | bytes 393216 | tf_op jit(solution)/shard_map/all_to_all | solution.py:76
Sparse Core Ops, SparseCore 0:
  88.9 72.7 reduce-scatter.2
  212.6 72.8 reduce-scatter.4
where the time goes:
time: 295 us; the launch traced here: 294 us
  waiting for transfers between devices  99 us (34%)
  blocking collectives  97.4 us (33%)
  matrix products  43.7 us (15%)
  local copies, waits for them, and re-layouts  29.5 us (10%)
  between operations  13.9 us (5%)
  starting transfers between devices  5.99 us (2%)
  other arithmetic  4.2 us (1%)
    reduce_scatter x2, waiting for transfers between devices, device_step(): lax.psum_scatter(shared_part, 'dp', scatter_dimension=0, tiled=True)  83 us
    all_gather x2, blocking collectives, device_step(): gathered = lax.all_gather(ffn_in, 'dp', axis=0, tiled=True)  62.3 us
    all_to_all x2, blocking collectives, device_step(): recv_buf = lax.all_to_all(send_buf, 'dp', 0, 0, tiled=True)  35.1 us
    squeeze x1, local copies, waits for them, and re-layouts, device_step(): cache[layer_idx]  25.4 us
    sub x2, matrix products, local_attention(): jax.nn.softmax(jnp.where(valid, scores, -jnp.inf), axis=-1)  18.4 us
    dot_general x2, matrix products, local_attention(): jnp.einsum('bht,btc->bhc', probs, cache_l[:, :, :LATENT], preferred_eleme...  16.4 us
    all_to_all x2, waiting for transfers between devices, device_step(): returned = lax.all_to_all(expert_out, 'dp', 0, 0, tiled=True)  15.8 us
  transfers between devices with their start and end apart: 4, of which 4 were waited for; matrix products, arithmetic and copies ran while one was open for 2% of the time, Pallas kernels for 0%

commit v1 on v0

v1 whole, which is shorter than its diff:
```python
import functools

import jax
import jax.numpy as jnp
from jax import lax
from jax.experimental import pallas as pl
from jax.experimental.pallas import tpu as pltpu
from jax.sharding import PartitionSpec as P

NORM_EPS = 1e-6
ATT_SCALE = 1.0 / (192.0 ** 0.5)
LATENT = 512
GROUP_SEQS = 8
SLOT_ROWS = 8
SHARD_ROWS = 16
F32 = jnp.float32
BF16 = jnp.bfloat16
MESH = pl.DeviceIdType.MESH
NT = (((1,), (1,)), ((), ()))


def rms_norm(vals32):
    return vals32 * lax.rsqrt(jnp.mean(vals32 * vals32, axis=-1, keepdims=True) + NORM_EPS)


def dot32(a, b):
    return jnp.dot(a, b, preferred_element_type=F32)


def dot_nt(a, b):
    return lax.dot_general(a, b, NT, preferred_element_type=F32)


def silu(v):
    return v * (1.0 / (1.0 + jnp.exp(-v)))


def step_kernel(
    group, lengths, x_ref, cache, w_q, w_o, ids_ref, slots_ref, rw_ref, w1e, w3e, w2e, w1s_ref, w3s_ref, w2s_ref,
    out_ref,
    cache_v, wq_v, wo_v, w1e_v, w3e_v, w2e_v, q_s, o_s, x_s, x1_s, ys_s,
    row_s, rwp_s, rwt_s, disp_s, sel_s, sh_send, sh_all, d_send, d_recv, r_send, r_recv,
    cache_sem, w_sem, sh_ssem, sh_rsem, d_ssem, d_rsem, r_ssem, r_rsem,
):
    me = lax.axis_index('dp')
    layers, batch = cache.shape[0], cache.shape[1]
    kv_dim = cache.shape[2]
    top_k = ids_ref.shape[0]
    local_experts = w1e.shape[1]
    shift = local_experts.bit_length() - 1
    d_model = x_ref.shape[1]
    n_rows = local_experts * group * SLOT_ROWS
    seq_len = cache.shape[3]

    def peer(i):
        return lax.rem(me + i, group)

    barrier = pltpu.get_barrier_semaphore()

    def greet(i, c):
        pl.semaphore_signal(barrier, inc=1, device_id={'dp': peer(i)}, device_id_type=MESH)
        return c

    lax.fori_loop(1, group, greet, 0)

    weight_copies = [
        pltpu.make_async_copy(src, dst, w_sem.at[i])
        for i, (src, dst) in enumerate(((w_q, wq_v), (w_o, wo_v), (w1e, w1e_v), (w3e, w3e_v), (w2e, w2e_v)))
    ]

    def cache_copy(l, b):
        return pltpu.make_async_copy(cache.at[l, b], cache_v.at[l, b], cache_sem.at[l, b])

    def start_cache(b, c):
        cache_copy(0, b).start()
        return c

    weight_copies[0].start()
    lax.fori_loop(0, batch, start_cache, 0)
    for cp in weight_copies[1:]:
        cp.start()

    for l in range(layers):
        for i, ref in enumerate((w1s_ref, w3s_ref, w2s_ref)):
            shard = ref[...].astype(F32)[:, l, :]
            sh_send[l, i] = jnp.zeros((SHARD_ROWS, d_model), BF16)
            sh_send[l, i, 0:shard.shape[0], :] = shard.astype(BF16)
            sh_all[l, i, me] = sh_send[l, i]
        ids = ids_ref[:, l, :]
        slots = slots_ref[:, l, :]
        rows = jnp.bitwise_and(ids, local_experts - 1) * (group * SLOT_ROWS) + jnp.right_shift(ids, shift) * SLOT_ROWS + slots
        rows = jnp.where(slots >= 0, rows, -1)
        r_iota = lax.broadcasted_iota(jnp.int32, (n_rows, batch), 0)
        disp = jnp.zeros((n_rows, batch), F32)
        for j in range(top_k):
            disp = jnp.where(r_iota == rows[j:j + 1, :], 1.0, disp)
        disp_s[l] = disp.astype(BF16)
        row_s[...] = jnp.full(row_s.shape, -1.0, F32)
        row_s[0:top_k, 0:batch] = rows.astype(F32)
        rwp_s[...] = jnp.zeros(rwp_s.shape, F32)
        rwp_s[0:top_k, 0:batch] = rw_ref[:, l, :]
        rows_t = row_s[...].T[0:batch, :]
        rwt_s[l] = rwp_s[...].T[0:batch, :]
        c_iota = lax.broadcasted_iota(jnp.int32, (batch, n_rows), 1).astype(F32)
        for j in range(top_k):
            sel_s[l, j * batch:(j + 1) * batch, :] = jnp.where(c_iota == rows_t[:, j:j + 1], 1.0, 0.0).astype(BF16)

    x_s[...] = x_ref[...].astype(F32)
    pl.semaphore_wait(barrier, group - 1)
    weight_copies[0].wait()

    row8 = jnp.bitwise_and(lax.broadcasted_iota(jnp.int32, (2 * GROUP_SEQS, seq_len), 0), GROUP_SEQS - 1)
    t_iota = lax.broadcasted_iota(jnp.int32, (2 * GROUP_SEQS, seq_len), 1)

    def sh_copy(l, i):
        return pltpu.make_async_remote_copy(
            src_ref=sh_send.at[l], dst_ref=sh_all.at[l, :, me], send_sem=sh_ssem.at[i], recv_sem=sh_rsem.at[i],
            device_id={'dp': peer(i)}, device_id_type=MESH)

    def d_copy(l, i):
        return pltpu.make_async_remote_copy(
            src_ref=d_send.at[l, :, peer(i)], dst_ref=d_recv.at[l, :, me], send_sem=d_ssem.at[i], recv_sem=d_rsem.at[i],
            device_id={'dp': peer(i)}, device_id_type=MESH)

    def r_copy(l, i):
        return pltpu.make_async_remote_copy(
            src_ref=r_send.at[l, :, peer(i)], dst_ref=r_recv.at[l, :, me], send_sem=r_ssem.at[i], recv_sem=r_rsem.at[i],
            device_id={'dp': peer(i)}, device_id_type=MESH)

    def each_peer(fn):
        def one(i, c):
            fn(i)
            return c
        lax.fori_loop(1, group, one, 0)

    def layer(l, carry):
        each_peer(lambda i: sh_copy(l, i).start())
        x = x_s[...]
        hidden = rms_norm(x).astype(BF16)
        q = dot32(hidden, wq_v[l]).astype(BF16).astype(F32)
        for g in range(batch // GROUP_SEQS):
            for h in range(2):
                q_s[g, h * GROUP_SEQS:(h + 1) * GROUP_SEQS, :] = q[g * GROUP_SEQS:(g + 1) * GROUP_SEQS, h * kv_dim:(h + 1) * kv_dim]

        def attend(g, c):
            qg = q_s[g].astype(BF16)
            base = g * GROUP_SEQS

            @pl.when(l + 1 < layers)
            def _():
                for j in range(GROUP_SEQS):
                    cache_copy(l + 1, base + j).start()

            s = jnp.full((2 * GROUP_SEQS, seq_len), -jnp.inf, F32)
            for j in range(GROUP_SEQS):
                cache_copy(l, base + j).wait()
                sj = dot32(qg, cache_v[l, base + j]) * ATT_SCALE
                keep = jnp.logical_and(row8 == j, t_iota < lengths[base + j])
                s = jnp.where(keep, sj, s)
            m = jnp.max(s, axis=-1, keepdims=True)
            e = jnp.exp(s - m)
            p = e * (1.0 / jnp.sum(e, axis=-1, keepdims=True))
            acc = jnp.zeros((LATENT, 2 * GROUP_SEQS), F32)
            for j in range(GROUP_SEQS):
                pj = jnp.where(row8 == j, p, 0.0).astype(BF16)
                acc = acc + dot_nt(cache_v[l, base + j, 0:LATENT, :], pj)
            og = acc.T
            rows_g = pl.ds(pl.multiple_of(base, GROUP_SEQS), GROUP_SEQS)
            o_s[rows_g, 0:LATENT] = og[0:GROUP_SEQS]
            o_s[rows_g, LATENT:2 * LATENT] = og[GROUP_SEQS:2 * GROUP_SEQS]
            return c

        lax.fori_loop(0, batch // GROUP_SEQS, attend, 0)

        @pl.when(l == 0)
        def _():
            for cp in weight_copies[1:]:
                cp.wait()

        x1 = (x + dot32(o_s[...].astype(BF16), wo_v[l])).astype(BF16).astype(F32)
        x1_s[...] = x1
        ffn_in = rms_norm(x1).astype(BF16)
        d_send[l] = dot32(disp_s[l], ffn_in).astype(BF16).reshape(local_experts, group, SLOT_ROWS, d_model)
        each_peer(lambda i: d_copy(l, i).start())
        d_recv[l, :, me] = d_send[l, :, me]

        each_peer(lambda i: sh_copy(l, i).wait_recv())
        hid = group * SHARD_ROWS
        up = dot_nt(ffn_in, sh_all[l, 0].reshape(hid, d_model))
        gate = dot_nt(ffn_in, sh_all[l, 1].reshape(hid, d_model))
        sh_h = (silu(gate) * up).astype(BF16)
        ys_s[...] = dot32(sh_h, sh_all[l, 2].reshape(hid, d_model))
        each_peer(lambda i: sh_copy(l, i).wait_send())

        each_peer(lambda i: d_copy(l, i).wait_recv())
        for n in range(local_experts):
            rows_in = d_recv[l, n].reshape(group * SLOT_ROWS, d_model)
            gate = dot_nt(rows_in, w3e_v[l, n])
            up = dot_nt(rows_in, w1e_v[l, n])
            eh = (silu(gate) * up).astype(BF16)
            r_send[l, n] = dot32(eh, w2e_v[l, n]).astype(BF16).reshape(group, SLOT_ROWS, d_model)
        each_peer(lambda i: r_copy(l, i).start())
        r_recv[l, :, me] = r_send[l, :, me]
        each_peer(lambda i: d_copy(l, i).wait_send())
        each_peer(lambda i: r_copy(l, i).wait_recv())
        picked = dot32(sel_s[l], r_recv[l].reshape(n_rows, d_model))
        rw = rwt_s[l]
        routed = rw[:, 0:1] * picked[0:batch]
        for j in range(1, top_k):
            routed = routed + rw[:, j:j + 1] * picked[j * batch:(j + 1) * batch]
        x_s[...] = (x1_s[...] + routed + ys_s[...]).astype(BF16).astype(F32)
        each_peer(lambda i: r_copy(l, i).wait_send())
        return carry

    lax.fori_loop(0, layers, layer, 0)
    out_ref[...] = x_s[...].astype(BF16)


def solution(mesh):
    group = mesh.shape['dp']
    tok_axes = ('replica', 'dp')
    in_specs = (
        P(tok_axes, None), P(tok_axes), P(None, tok_axes, None, None),
        P(None, None, None), P(None, None, None),
        P(None, tok_axes, None), P(None, tok_axes, None), P(None, tok_axes, None),
        P(None, 'dp', None, None), P(None, 'dp', None, None), P(None, 'dp', None, None),
        P(None, None, 'dp'), P(None, None, 'dp'), P(None, 'dp', None),
    )

    def device_step(x, lengths, cache, w_q, w_o, expert_ids, slots, route_w, w1_exp, w3_exp, w2_exp, w1_sh, w3_sh, w2_sh):
        batch, d_model = x.shape
        layers, _, seq_len, kv_dim = cache.shape
        local_experts, ff = w1_exp.shape[1], w1_exp.shape[3]
        top_k = expert_ids.shape[2]
        n_rows = local_experts * group * SLOT_ROWS
        vmem = pl.BlockSpec(memory_space=pltpu.VMEM)
        smem = pl.BlockSpec(memory_space=pltpu.SMEM)
        hbm = pl.BlockSpec(memory_space=pl.ANY)
        block = (layers, local_experts, group, SLOT_ROWS, d_model)
        scratch = [
            pltpu.VMEM((layers, batch, kv_dim, seq_len), BF16),
            pltpu.VMEM(w_q.shape, BF16),
            pltpu.VMEM(w_o.shape, BF16),
            pltpu.VMEM((layers, local_experts, ff, d_model), BF16),
            pltpu.VMEM((layers, local_experts, ff, d_model), BF16),
            pltpu.VMEM((layers, local_experts, ff, d_model), BF16),
            pltpu.VMEM((batch // GROUP_SEQS, 2 * GROUP_SEQS, kv_dim), F32),
            pltpu.VMEM((batch, 2 * LATENT), F32),
            pltpu.VMEM((batch, d_model), F32),
            pltpu.VMEM((batch, d_model), F32),
            pltpu.VMEM((batch, d_model), F32),
            pltpu.VMEM((8, 128), F32),
            pltpu.VMEM((8, 128), F32),
            pltpu.VMEM((layers, batch, 8), F32),
            pltpu.VMEM((layers, n_rows, batch), BF16),
            pltpu.VMEM((layers, top_k * batch, n_rows), BF16),
            pltpu.VMEM((layers, 3, SHARD_ROWS, d_model), BF16),
            pltpu.VMEM((layers, 3, group, SHARD_ROWS, d_model), BF16),
            pltpu.VMEM(block, BF16),
            pltpu.VMEM(block, BF16),
            pltpu.VMEM(block, BF16),
            pltpu.VMEM(block, BF16),
            pltpu.SemaphoreType.DMA((layers, batch)),
            pltpu.SemaphoreType.DMA((5,)),
        ] + [pltpu.SemaphoreType.DMA((group,))] * 6
        return pl.pallas_call(
            functools.partial(step_kernel, group),
            out_shape=jax.ShapeDtypeStruct((batch, d_model), BF16),
            in_specs=[smem, vmem, hbm, hbm, hbm, vmem, vmem, vmem, hbm, hbm, hbm, vmem, vmem, vmem],
            out_specs=vmem,
            scratch_shapes=scratch,
            compiler_params=pltpu.CompilerParams(collective_id=0, has_side_effects=True, vmem_limit_bytes=62 * 1024 * 1024),
        )(
            lengths, x, jnp.swapaxes(cache, 2, 3), w_q, w_o,
            jnp.transpose(expert_ids, (2, 0, 1)), jnp.transpose(slots, (2, 0, 1)), jnp.transpose(route_w, (2, 0, 1)),
            jnp.swapaxes(w1_exp, 2, 3), jnp.swapaxes(w3_exp, 2, 3), w2_exp,
            jnp.transpose(w1_sh, (2, 0, 1)), jnp.transpose(w3_sh, (2, 0, 1)), jnp.transpose(w2_sh, (1, 0, 2)),
        )

    return jax.shard_map(device_step, mesh=mesh, in_specs=in_specs, out_specs=P(tok_axes, None), check_vma=False)
```

time: 295 us -> 67.8 us (0.23)
  waiting for transfers between devices: 99 us -> 0 us
  blocking collectives: 97.4 us -> 0 us
  Pallas kernels: 0 us -> 66.2 us
  matrix products: 43.7 us -> 0 us
  local copies, waits for them, and re-layouts: 29.5 us -> 1.32 us
  between operations: 13.9 us -> 0.01 us
  starting transfers between devices: 5.99 us -> 0 us
  other arithmetic: 4.2 us -> 0 us
    reduce_scatter x2 -> x0, waiting for transfers between devices: 83 us -> none  [device_step(): lax.psum_scatter(shared_part, 'dp', scatter_dimension=0, tiled=True)]
    pallas_call x0 -> x1, Pallas kernels: none -> 66.2 us  [device_step(): pl.pallas_call(functools.partial(step_kernel, group), out_shape=jax.Shape...]
    all_gather x2 -> x0, blocking collectives: 62.3 us -> none  [device_step(): gathered = lax.all_gather(ffn_in, 'dp', axis=0, tiled=True)]
    all_to_all x2 -> x0, blocking collectives: 35.1 us -> none  [device_step(): recv_buf = lax.all_to_all(send_buf, 'dp', 0, 0, tiled=True)]
    squeeze x1 -> x0, local copies, waits for them, and re-layouts: 25.4 us -> none  [device_step(): cache[layer_idx]]
    dot_general x18 -> x0, matrix products: 25.3 us -> none  [the longest x2 16.4 us: local_attention(): jnp.einsum('bht,btc->bhc', probs, cache_l[:, :, :LATENT], preferred_eleme...]
    sub x2 -> x0, matrix products: 18.4 us -> none  [local_attention(): jax.nn.softmax(jnp.where(valid, scores, -jnp.inf), axis=-1)]
    all_to_all x2 -> x0, waiting for transfers between devices: 15.8 us -> none  [device_step(): returned = lax.all_to_all(expert_out, 'dp', 0, 0, tiled=True)]
  transfers between devices with their start and end apart: 4 -> 0, of which waited for: 4 -> 0; matrix products, arithmetic and copies ran while one was open for 2% -> 0% of each run, Pallas kernels for 0% -> 0%
where the time goes in v1:
time: 67.8 us; the launch traced here: 67.5 us
  Pallas kernels  66.2 us (98%)
  local copies, waits for them, and re-layouts  1.32 us (2%)
    pallas_call x1, Pallas kernels, device_step(): pl.pallas_call(functools.partial(step_kernel, group), out_shape=jax.Shape...  66.2 us

profile of v1, /device:TPU:97, one launch (start us, length us, event | category | flops | bytes accessed | tf_op | source)
XLA Modules:
  0.0 67.5 jit_solution(16746204256309723931)
XLA Ops:
  0.0 66.2 %shard_map.136 = bf16[32,256]{1,0:T(8,128)(2,1)} custom-call(s32[32]{0:T(128)} %lengths.1, bf16[32,256]{1,0:T(8,128)(2,1)} %x_ref.1, bf16[2,32,576,512]{3,2,1,0:T(8,128)(2,1)} %bitcast.9, bf16[2,256,1152]{2,1,0:T(8,128)(2,1)} %w_q.1, bf16[2,1024,256]{2,1,0:T(8,128)(2,1)} %w_o.1, s32[6,2,32]{2,1,0:T(2,128)} %bitcast.15, s32[6,2,32]{2,1,0:T(2,128)} %bitcast.16, ...), custom_call_target="tpu_custom_call" | custom-call | tf_op jit(solution)/shard_map/pallas_call | solution.py:266
  66.2 1.3 %copy.16 = bf16[32,256]{1,0:T(8,128)(2,1)} copy(bf16[32,256]{1,0:T(8,128)(2,1)} %shard_map.136) | data formatting | bytes 32768

commit v2 on v1

v2 whole, which is shorter than its diff:
```python
import functools

import jax
import jax.numpy as jnp
from jax import lax
from jax.experimental import pallas as pl
from jax.experimental.pallas import tpu as pltpu
from jax.sharding import PartitionSpec as P

NORM_EPS = 1e-6
ATT_SCALE = 1.0 / (192.0 ** 0.5)
LATENT = 512
GROUP_SEQS = 8
SLOT_ROWS = 8
SHARD_ROWS = 16
F32 = jnp.float32
BF16 = jnp.bfloat16
MESH = pl.DeviceIdType.MESH
NT = (((1,), (1,)), ((), ()))


def rms_norm(vals32):
    return vals32 * lax.rsqrt(jnp.mean(vals32 * vals32, axis=-1, keepdims=True) + NORM_EPS)


def dot32(a, b):
    return jnp.dot(a, b, preferred_element_type=F32)


def dot_nt(a, b):
    return lax.dot_general(a, b, NT, preferred_element_type=F32)


def silu(v):
    return v * (1.0 / (1.0 + jnp.exp(-v)))


def step_kernel(
    group, side, lengths, x_in, cache, w_q, w_o, ids_in, slots_in, rw_in, w1e, w3e, w2e, w1s, w3s, w2s,
    out_ref,
    len_s, x_v, ids_v, slots_v, rw_v, shard_v, cache_v, wq_v, wo_v, w1e_v, w3e_v, w2e_v, q_s, p_s, o_s, x_s, x1_s,
    row_s, rwp_s, rwt_s, disp_s, sel_s, sh_send, sh_all, d_send, d_recv, r_send, r_recv,
    cache_sem, in_sem, sh_ssem, sh_rsem, d_ssem, d_rsem, r_ssem, r_rsem,
):
    me = lax.axis_index('dp')
    core = lax.rem(me, 2)
    chip_x = lax.rem(me // 2, side)
    chip_y = me // (2 * side)
    layers, batch, kv_dim, seq_len = cache.shape
    top_k = ids_in.shape[0]
    local_experts = w1e.shape[1]
    shift = local_experts.bit_length() - 1
    d_model = x_in.shape[1]
    n_rows = local_experts * group * SLOT_ROWS
    n_groups = batch // GROUP_SEQS
    used = pl.ds(0, max(1, 2 * batch * top_k // (local_experts * group)))

    def at_offset(dy, dx, dc):
        return (lax.rem(chip_y + dy, side) * side + lax.rem(chip_x + dx, side)) * 2 + lax.rem(core + dc, 2)

    def far(offset):
        return -(min(offset[0], side - offset[0]) + min(offset[1], side - offset[1])), -offset[2]

    offsets = [(dy, dx, dc) for dy in range(side) for dx in range(side) for dc in range(2)]
    offsets = sorted(offsets, key=far)[:-1]
    assert side == 4

    row_a = chip_y + core * (chip_x - chip_y)
    col_b = chip_x + core * (chip_y - chip_x)

    def device_at(a, b):
        return ((a + core * (b - a)) * side + (b + core * (a - b))) * 2 + core

    copies = {
        name: pltpu.make_async_copy(src, dst, in_sem.at[i])
        for i, (name, src, dst) in enumerate((
            ('x', x_in, x_v), ('wq0', w_q.at[0], wq_v.at[0]), ('len', lengths, len_s),
            ('s0', w1s, shard_v.at[0]), ('s1', w3s, shard_v.at[1]), ('s2', w2s, shard_v.at[2]),
            ('ids', ids_in, ids_v), ('slots', slots_in, slots_v), ('rw', rw_in, rw_v),
            ('wo', w_o, wo_v), ('w1e', w1e, w1e_v), ('w3e', w3e, w3e_v), ('w2e', w2e, w2e_v),
            ('wq1', w_q.at[1:], wq_v.at[1:]),
        ))
    }

    def start_group(l, g):
        for j in range(GROUP_SEQS):
            b = g * GROUP_SEQS + j
            pltpu.make_async_copy(cache.at[l, b], cache_v.at[l, b], cache_sem.at[l, g]).start()

    def wait_group(l, g):
        rows = pl.ds(g * GROUP_SEQS, GROUP_SEQS)
        pltpu.make_async_copy(cache.at[l, rows], cache_v.at[l, rows], cache_sem.at[l, g]).wait()

    def start_layer(l, first=0):
        def one(g, c):
            start_group(l, g)
            return c
        lax.fori_loop(first, n_groups, one, 0)

    for name in ('x', 'wq0', 'len'):
        copies[name].start()
    start_group(0, 0)
    for name in ('s0', 's1', 's2', 'ids', 'slots'):
        copies[name].start()
    r_recv[...] = jnp.zeros(r_recv.shape, BF16)

    barrier = pltpu.get_barrier_semaphore()

    def greet(i, c):
        pl.semaphore_signal(barrier, inc=1, device_id={'dp': lax.rem(me + i, group)}, device_id_type=MESH)
        return c

    lax.fori_loop(1, group, greet, 0)
    start_layer(0, 1)
    for name in ('rw', 'wo', 'w1e', 'w3e', 'w2e', 'wq1'):
        copies[name].start()

    for i in range(3):
        copies[f's{i}'].wait()
    for i in range(3):
        shards = shard_v[i].astype(F32)
        for l in range(layers):
            sh_send[l, i] = jnp.zeros((SHARD_ROWS, d_model), BF16)
            sh_send[l, i, 0:shards.shape[0], :] = shards[:, l, :].astype(BF16)
    copies['ids'].wait()
    copies['slots'].wait()

    def routed_rows(l):
        ids = ids_v[:, l, :]
        slots = slots_v[:, l, :]
        rows = jnp.bitwise_and(ids, local_experts - 1) * (group * SLOT_ROWS) + jnp.right_shift(ids, shift) * SLOT_ROWS + slots
        return jnp.where(slots >= 0, rows, -1)

    def build_dispatch(l):
        rows = routed_rows(l)
        r_iota = lax.broadcasted_iota(jnp.int32, (n_rows, batch), 0)
        disp = jnp.zeros((n_rows, batch), F32)
        for j in range(top_k):
            disp = jnp.where(r_iota == rows[j:j + 1, :], 1.0, disp)
        disp_s[l] = disp.astype(BF16)

    def build_select(l):
        row_s[...] = jnp.full(row_s.shape, -1.0, F32)
        row_s[0:top_k, 0:batch] = routed_rows(l).astype(F32)
        rwp_s[...] = jnp.zeros(rwp_s.shape, F32)
        rwp_s[0:top_k, 0:batch] = rw_v[:, l, :]
        rows_t = row_s[...].T[0:batch, :]
        rwt_s[l] = rwp_s[...].T[0:batch, :]
        c_iota = lax.broadcasted_iota(jnp.int32, (batch, n_rows), 1).astype(F32)
        for j in range(top_k):
            sel_s[l, j * batch:(j + 1) * batch, :] = jnp.where(c_iota == rows_t[:, j:j + 1], 1.0, 0.0).astype(BF16)

    build_dispatch(0)
    copies['x'].wait()
    copies['wq0'].wait()
    copies['len'].wait()
    x_s[...] = x_v[...].astype(F32)

    row8 = jnp.bitwise_and(lax.broadcasted_iota(jnp.int32, (2 * GROUP_SEQS, seq_len), 0), GROUP_SEQS - 1)
    row8v = jnp.bitwise_and(lax.broadcasted_iota(jnp.int32, (2 * GROUP_SEQS, LATENT), 0), GROUP_SEQS - 1)
    t_iota = lax.broadcasted_iota(jnp.int32, (2 * GROUP_SEQS, seq_len), 1)

    def remote(src, dst, ssem, rsem, dev):
        return pltpu.make_async_remote_copy(
            src_ref=src, dst_ref=dst, send_sem=ssem, recv_sem=rsem, device_id={'dp': dev}, device_id_type=MESH)

    def wait_block(ref, sem):
        pltpu.make_async_copy(ref, ref, sem).wait()

    def wait_all_peers(ref, sem):
        wait_block(ref.at[:, pl.ds(0, group - 1), used], sem)

    def spread_1(l):
        sh_all[l, core, row_a, col_b] = sh_send[l]
        for k in (2, 1, 3):
            dev = device_at(row_a, lax.rem(col_b + k, side))
            remote(sh_send.at[l], sh_all.at[l, core, row_a, col_b], sh_ssem.at[0], sh_rsem.at[0], dev).start()

    def spread_2(l):
        wait_block(sh_all.at[l, 0, 0, pl.ds(0, side - 1)], sh_rsem.at[0])
        line = sh_all.at[l, core, row_a]
        for k in (1, side - 1):
            dev = device_at(lax.rem(row_a + k, side), col_b)
            remote(line, line, sh_ssem.at[1], sh_rsem.at[1], dev).start()

    def spread_3(l):
        wait_block(sh_all.at[l, 0, pl.ds(0, 2)], sh_rsem.at[1])
        for k, half in ((1, 0), (side - 1, side // 2)):
            dev = device_at(lax.rem(row_a + k, side), col_b)
            part = sh_all.at[l, core, lax.rem(row_a + side - k, side), pl.ds(half, side // 2)]
            remote(part, part, sh_ssem.at[2], sh_rsem.at[2], dev).start()

    def spread_4(l):
        wait_block(sh_all.at[l, 0, 0], sh_rsem.at[2])
        half = sh_all.at[l, core]
        remote(half, half, sh_ssem.at[3], sh_rsem.at[3], me + 1 - 2 * core).start()

    def spread_end(l):
        wait_block(sh_all.at[l, 0], sh_rsem.at[3])
        wait_block(sh_all.at[l, 0, 0, pl.ds(0, side - 1)], sh_ssem.at[0])
        wait_block(sh_all.at[l, 0, pl.ds(0, 2)], sh_ssem.at[1])
        wait_block(sh_all.at[l, 0, 0], sh_ssem.at[2])
        wait_block(sh_all.at[l, 0], sh_ssem.at[3])

    def layer(l, carry):
        x = x_s[...]
        hidden = rms_norm(x).astype(BF16)
        q = dot32(hidden, wq_v[l]).astype(BF16).astype(F32)
        for g in range(n_groups):
            for h in range(2):
                q_s[g, h * GROUP_SEQS:(h + 1) * GROUP_SEQS, :] = q[g * GROUP_SEQS:(g + 1) * GROUP_SEQS, h * kv_dim:(h + 1) * kv_dim]

        def score_step(s, qg, g, j):
            sj = dot32(qg, cache_v[l, g * GROUP_SEQS + j]) * ATT_SCALE
            keep = jnp.logical_and(row8 == j, t_iota < len_s[g * GROUP_SEQS + j])
            return jnp.where(keep, sj, s)

        def softmax(s):
            e = jnp.exp(s - jnp.max(s, axis=-1, keepdims=True))
            return e * (1.0 / jnp.sum(e, axis=-1, keepdims=True))

        def value_step(acc, p, g, j):
            return jnp.where(row8v == j, dot_nt(p, cache_v[l, g * GROUP_SEQS + j, 0:LATENT, :]), acc)

        def put_out(acc, g):
            og = acc
            rows_g = pl.ds(pl.multiple_of(g * GROUP_SEQS, GROUP_SEQS), GROUP_SEQS)
            o_s[rows_g, 0:LATENT] = og[0:GROUP_SEQS]
            o_s[rows_g, LATENT:2 * LATENT] = og[GROUP_SEQS:2 * GROUP_SEQS]

        no_score = jnp.full((2 * GROUP_SEQS, seq_len), -jnp.inf, F32)
        no_out = jnp.zeros((2 * GROUP_SEQS, LATENT), F32)

        wait_group(l, 0)
        s = no_score
        qg = q_s[0].astype(BF16)
        for j in range(GROUP_SEQS):
            s = score_step(s, qg, 0, j)
        p_s[...] = softmax(s)

        @pl.when(l == 0)
        def _():
            pl.semaphore_wait(barrier, group - 1)

        spread_1(l)

        def attend(g, c):
            wait_group(l, g + 1)
            p = p_s[...].astype(BF16)
            qg = q_s[g + 1].astype(BF16)
            s, acc = no_score, no_out
            for j in range(GROUP_SEQS):
                s = score_step(s, qg, g + 1, j)
                acc = value_step(acc, p, g, j)
            p_s[...] = softmax(s)
            put_out(acc, g)
            @pl.when(g == n_groups // 2 - 1)
            def _():
                spread_2(l)
            return c

        lax.fori_loop(0, n_groups - 1, attend, 0)
        p = p_s[...].astype(BF16)
        acc = no_out
        for j in range(GROUP_SEQS):
            acc = value_step(acc, p, n_groups - 1, j)
        put_out(acc, n_groups - 1)

        @pl.when(l == 0)
        def _():
            for name in ('wo', 'w1e', 'w3e', 'w2e', 'wq1', 'rw'):
                copies[name].wait()

        x1 = (x_s[...] + dot32(o_s[...].astype(BF16), wo_v[l])).astype(BF16).astype(F32)
        x1_s[...] = x1
        ffn_in = rms_norm(x1).astype(BF16)
        d_send[l] = dot32(disp_s[l], ffn_in).astype(BF16).reshape(local_experts, group, SLOT_ROWS, d_model)
        for off in offsets:
            dev = at_offset(*off)
            remote(d_send.at[l, :, dev, used], d_recv.at[l, :, me, used], d_ssem.at[0], d_rsem.at[0], dev).start()
        d_recv[l, :, me] = d_send[l, :, me]
        spread_3(l)

        @pl.when(l + 1 < layers)
        def _():
            start_layer(l + 1)

        @pl.when(l == 0)
        def _():
            for other in range(1, layers):
                build_dispatch(other)
            for other in range(layers):
                build_select(other)

        wait_all_peers(d_recv.at[l], d_rsem.at[0])
        spread_4(l)
        for n in range(local_experts):
            rows_in = d_recv[l, n].reshape(group * SLOT_ROWS, d_model)
            gate = dot_nt(rows_in, w3e_v[l, n])
            up = dot_nt(rows_in, w1e_v[l, n])
            eh = (silu(gate) * up).astype(BF16)
            r_send[l, n] = dot32(eh, w2e_v[l, n]).astype(BF16).reshape(group, SLOT_ROWS, d_model)
        for off in offsets:
            dev = at_offset(*off)
            remote(r_send.at[l, :, dev, used], r_recv.at[l, :, me, used], r_ssem.at[0], r_rsem.at[0], dev).start()
        r_recv[l, :, me] = r_send[l, :, me]
        spread_end(l)
        hid = group * SHARD_ROWS
        ffn_in = rms_norm(x1_s[...]).astype(BF16)
        up = dot_nt(ffn_in, sh_all[l, :, :, :, 0].reshape(hid, d_model))
        gate = dot_nt(ffn_in, sh_all[l, :, :, :, 1].reshape(hid, d_model))
        sh_h = (silu(gate) * up).astype(BF16)
        x1_s[...] = x1_s[...] + dot32(sh_h, sh_all[l, :, :, :, 2].reshape(hid, d_model))
        wait_all_peers(d_send.at[l], d_ssem.at[0])
        wait_all_peers(r_recv.at[l], r_rsem.at[0])
        picked = dot32(sel_s[l], r_recv[l].reshape(n_rows, d_model))
        rw = rwt_s[l]
        routed = rw[:, 0:1] * picked[0:batch]
        for j in range(1, top_k):
            routed = routed + rw[:, j:j + 1] * picked[j * batch:(j + 1) * batch]
        x_s[...] = (x1_s[...] + routed).astype(BF16).astype(F32)
        wait_all_peers(r_send.at[l], r_ssem.at[0])
        return carry

    lax.fori_loop(0, layers, layer, 0)
    out_ref[...] = x_s[...].astype(BF16)


def solution(mesh):
    group = mesh.shape['dp']
    side = 1
    while 2 * side * side < group:
        side += 1
    tok_axes = ('replica', 'dp')
    in_specs = (
        P(tok_axes, None), P(tok_axes), P(None, tok_axes, None, None),
        P(None, None, None), P(None, None, None),
        P(None, tok_axes, None), P(None, tok_axes, None), P(None, tok_axes, None),
        P(None, 'dp', None, None), P(None, 'dp', None, None), P(None, 'dp', None, None),
        P(None, None, 'dp'), P(None, None, 'dp'), P(None, 'dp', None),
    )

    def device_step(x, lengths, cache, w_q, w_o, expert_ids, slots, route_w, w1_exp, w3_exp, w2_exp, w1_sh, w3_sh, w2_sh):
        batch, d_model = x.shape
        layers, _, seq_len, kv_dim = cache.shape
        local_experts, ff = w1_exp.shape[1], w1_exp.shape[3]
        top_k = expert_ids.shape[2]
        n_rows = local_experts * group * SLOT_ROWS
        vmem = pl.BlockSpec(memory_space=pltpu.VMEM)
        hbm = pl.BlockSpec(memory_space=pl.ANY)
        block = (layers, local_experts, group, SLOT_ROWS, d_model)
        expert = (layers, local_experts, ff, d_model)
        route = (top_k, layers, batch)
        one_sem = pltpu.SemaphoreType.DMA((1,))
        scratch = [
            pltpu.SMEM((batch,), jnp.int32),
            pltpu.VMEM((batch, d_model), BF16),
            pltpu.VMEM(route, jnp.int32),
            pltpu.VMEM(route, jnp.int32),
            pltpu.VMEM(route, F32),
            pltpu.VMEM((3, w1_sh.shape[2], layers, d_model), BF16),
            pltpu.VMEM((layers, batch, kv_dim, seq_len), BF16),
            pltpu.VMEM(w_q.shape, BF16),
            pltpu.VMEM(w_o.shape, BF16),
            pltpu.VMEM(expert, BF16),
            pltpu.VMEM(expert, BF16),
            pltpu.VMEM(expert, BF16),
            pltpu.VMEM((batch // GROUP_SEQS, 2 * GROUP_SEQS, kv_dim), F32),
            pltpu.VMEM((2 * GROUP_SEQS, seq_len), F32),
            pltpu.VMEM((batch, 2 * LATENT), F32),
            pltpu.VMEM((batch, d_model), F32),
            pltpu.VMEM((batch, d_model), F32),
            pltpu.VMEM((8, 128), F32),
            pltpu.VMEM((8, 128), F32),
            pltpu.VMEM((layers, batch, 8), F32),
            pltpu.VMEM((layers, n_rows, batch), BF16),
            pltpu.VMEM((layers, top_k * batch, n_rows), BF16),
            pltpu.VMEM((layers, 3, SHARD_ROWS, d_model), BF16),
            pltpu.VMEM((layers, 2, side, side, 3, SHARD_ROWS, d_model), BF16),
            pltpu.VMEM(block, BF16),
            pltpu.VMEM(block, BF16),
            pltpu.VMEM(block, BF16),
            pltpu.VMEM(block, BF16),
            pltpu.SemaphoreType.DMA((layers, batch // GROUP_SEQS)),
            pltpu.SemaphoreType.DMA((14,)),
            pltpu.SemaphoreType.DMA((4,)),
            pltpu.SemaphoreType.DMA((4,)),
            one_sem, one_sem, one_sem, one_sem,
        ]
        return pl.pallas_call(
            functools.partial(step_kernel, group, side),
            out_shape=jax.ShapeDtypeStruct((batch, d_model), BF16),
            in_specs=[hbm] * 14,
            out_specs=vmem,
            scratch_shapes=scratch,
            compiler_params=pltpu.CompilerParams(collective_id=0, has_side_effects=True, vmem_limit_bytes=60 * 1024 * 1024),
        )(
            lengths, x, jnp.swapaxes(cache, 2, 3), w_q, w_o,
            jnp.transpose(expert_ids, (2, 0, 1)), jnp.transpose(slots, (2, 0, 1)), jnp.transpose(route_w, (2, 0, 1)),
            jnp.swapaxes(w1_exp, 2, 3), jnp.swapaxes(w3_exp, 2, 3), w2_exp,
            jnp.transpose(w1_sh, (2, 0, 1)), jnp.transpose(w3_sh, (2, 0, 1)), jnp.transpose(w2_sh, (1, 0, 2)),
        )

    return jax.shard_map(device_step, mesh=mesh, in_specs=in_specs, out_specs=P(tok_axes, None), check_vma=False)
```

time: 67.8 us -> 50.8 us (0.75)
  Pallas kernels: 66.2 us -> 49.3 us
    pallas_call x1, Pallas kernels: 66.2 us -> 49.3 us  [device_step(): pl.pallas_call(functools.partial(step_kernel, group, side), out_shape=jax...]
where the time goes in v2:
time: 50.8 us; the launch traced here: 50.6 us
  Pallas kernels  49.3 us (97%)
  local copies, waits for them, and re-layouts  1.32 us (3%)
    pallas_call x1, Pallas kernels, device_step(): pl.pallas_call(functools.partial(step_kernel, group, side), out_shape=jax...  49.3 us
    unnamed x1, local copies, waits for them, and re-layouts  1.32 us

profile of v2, /device:TPU:97, one launch (start us, length us, event | category | flops | bytes accessed | tf_op | source)
XLA Modules:
  0.0 50.6 jit_solution(16523237116806870107)
XLA Ops:
  0.0 49.3 %shard_map.136 = bf16[32,256]{1,0:T(8,128)(2,1)} custom-call(s32[32]{0:T(128)} %lengths.1, bf16[32,256]{1,0:T(8,128)(2,1)} %x_in.1, bf16[2,32,576,512]{3,2,1,0:T(8,128)(2,1)} %bitcast.9, bf16[2,256,1152]{2,1,0:T(8,128)(2,1)} %w_q.1, bf16[2,1024,256]{2,1,0:T(8,128)(2,1)} %w_o.1, s32[6,2,32]{2,1,0:T(2,128)} %bitcast.15, s32[6,2,32]{2,1,0:T(2,128)} %bitcast.16, ...), custom_call_target="tpu_custom_call" | custom-call | tf_op jit(solution)/shard_map/pallas_call | solution.py:390
  49.3 1.3 %copy.16 = bf16[32,256]{1,0:T(8,128)(2,1)} copy(bf16[32,256]{1,0:T(8,128)(2,1)} %shard_map.136) | data formatting | bytes 32768

commit v3 on v2

--- a/solution.py
+++ b/solution.py
@@ -11,6 +11,8 @@
 ATT_SCALE = 1.0 / (192.0 ** 0.5)
 LATENT = 512
 GROUP_SEQS = 8
+HALF = 4
+TURNED = 5
 SLOT_ROWS = 8
 SHARD_ROWS = 16
 F32 = jnp.float32
@@ -39,7 +41,7 @@
     group, side, lengths, x_in, cache, w_q, w_o, ids_in, slots_in, rw_in, w1e, w3e, w2e, w1s, w3s, w2s,
     out_ref,
     len_s, x_v, ids_v, slots_v, rw_v, shard_v, cache_v, wq_v, wo_v, w1e_v, w3e_v, w2e_v, q_s, p_s, o_s, x_s, x1_s,
-    row_s, rwp_s, rwt_s, disp_s, sel_s, sh_send, sh_all, d_send, d_recv, r_send, r_recv,
+    turn_s, row_s, rwp_s, rwt_s, disp_s, sel_s, sh_send, sh_all, d_send, d_recv, r_send, r_recv,
     cache_sem, in_sem, sh_ssem, sh_rsem, d_ssem, d_rsem, r_ssem, r_rsem,
 ):
     me = lax.axis_index('dp')
@@ -63,7 +65,7 @@
 
     offsets = [(dy, dx, dc) for dy in range(side) for dx in range(side) for dc in range(2)]
     offsets = sorted(offsets, key=far)[:-1]
-    assert side == 4
+    assert side == 4 and layers == 2
 
     row_a = chip_y + core * (chip_x - chip_y)
     col_b = chip_x + core * (chip_y - chip_x)
@@ -82,26 +84,31 @@
         ))
     }
 
-    def start_group(l, g):
-        for j in range(GROUP_SEQS):
-            b = g * GROUP_SEQS + j
-            pltpu.make_async_copy(cache.at[l, b], cache_v.at[l, b], cache_sem.at[l, g]).start()
+    def start_half(l, k):
+        def one(j, c):
+            b = k * HALF + j
+            pltpu.make_async_copy(cache.at[l, b], cache_v.at[l, b], cache_sem.at[l, k]).start()
+            return c
+        lax.fori_loop(0, HALF, one, 0, unroll=True)
+
+    def start_halves(l, first, last):
+        def one(k, c):
+            start_half(l, k)
+            return c
+        lax.fori_loop(first, last, one, 0)
+
+    def wait_half(l, k):
+        rows = pl.ds(k * HALF, HALF)
+        pltpu.make_async_copy(cache.at[l, rows], cache_v.at[l, rows], cache_sem.at[l, k]).wait()
 
     def wait_group(l, g):
-        rows = pl.ds(g * GROUP_SEQS, GROUP_SEQS)
-        pltpu.make_async_copy(cache.at[l, rows], cache_v.at[l, rows], cache_sem.at[l, g]).wait()
-
-    def start_layer(l, first=0):
-        def one(g, c):
-            start_group(l, g)
-            return c
-        lax.fori_loop(first, n_groups, one, 0)
-
-    for name in ('x', 'wq0', 'len'):
+        wait_half(l, 2 * g)
+        wait_half(l, 2 * g + 1)
+
+    n_halves = batch // HALF
+    for name in ('x', 's0', 's1', 's2', 'ids', 'slots', 'len', 'wq0'):
         copies[name].start()
-    start_group(0, 0)
-    for name in ('s0', 's1', 's2', 'ids', 'slots'):
-        copies[name].start()
+    start_half(0, 0)
     r_recv[...] = jnp.zeros(r_recv.shape, BF16)
 
     barrier = pltpu.get_barrier_semaphore()
@@ -111,7 +118,7 @@
         return c
 
     lax.fori_loop(1, group, greet, 0)
-    start_layer(0, 1)
+    start_halves(0, 1, n_halves)
     for name in ('rw', 'wo', 'w1e', 'w3e', 'w2e', 'wq1'):
         copies[name].start()
 
@@ -174,35 +181,50 @@
         sh_all[l, core, row_a, col_b] = sh_send[l]
         for k in (2, 1, 3):
             dev = device_at(row_a, lax.rem(col_b + k, side))
-            remote(sh_send.at[l], sh_all.at[l, core, row_a, col_b], sh_ssem.at[0], sh_rsem.at[0], dev).start()
+            remote(sh_send.at[l], sh_all.at[l, core, row_a, col_b], sh_ssem.at[l, 0], sh_rsem.at[l, 0], dev).start()
 
     def spread_2(l):
-        wait_block(sh_all.at[l, 0, 0, pl.ds(0, side - 1)], sh_rsem.at[0])
+        wait_block(sh_all.at[l, 0, 0, pl.ds(0, side - 1)], sh_rsem.at[l, 0])
         line = sh_all.at[l, core, row_a]
         for k in (1, side - 1):
             dev = device_at(lax.rem(row_a + k, side), col_b)
-            remote(line, line, sh_ssem.at[1], sh_rsem.at[1], dev).start()
+            remote(line, line, sh_ssem.at[l, 1], sh_rsem.at[l, 1], dev).start()
 
     def spread_3(l):
-        wait_block(sh_all.at[l, 0, pl.ds(0, 2)], sh_rsem.at[1])
+        wait_block(sh_all.at[l, 0, pl.ds(0, 2)], sh_rsem.at[l, 1])
         for k, half in ((1, 0), (side - 1, side // 2)):
             dev = device_at(lax.rem(row_a + k, side), col_b)
             part = sh_all.at[l, core, lax.rem(row_a + side - k, side), pl.ds(half, side // 2)]
-            remote(part, part, sh_ssem.at[2], sh_rsem.at[2], dev).start()
+            remote(part, part, sh_ssem.at[l, 2], sh_rsem.at[l, 2], dev).start()
 
     def spread_4(l):
-        wait_block(sh_all.at[l, 0, 0], sh_rsem.at[2])
+        wait_block(sh_all.at[l, 0, 0], sh_rsem.at[l, 2])
         half = sh_all.at[l, core]
-        remote(half, half, sh_ssem.at[3], sh_rsem.at[3], me + 1 - 2 * core).start()
+        remote(half, half, sh_ssem.at[l, 3], sh_rsem.at[l, 3], me + 1 - 2 * core).start()
 
     def spread_end(l):
-        wait_block(sh_all.at[l, 0], sh_rsem.at[3])
-        wait_block(sh_all.at[l, 0, 0, pl.ds(0, side - 1)], sh_ssem.at[0])
-        wait_block(sh_all.at[l, 0, pl.ds(0, 2)], sh_ssem.at[1])
-        wait_block(sh_all.at[l, 0, 0], sh_ssem.at[2])
-        wait_block(sh_all.at[l, 0], sh_ssem.at[3])
-
-    def layer(l, carry):
+        wait_block(sh_all.at[l, 0], sh_rsem.at[l, 3])
+        wait_block(sh_all.at[l, 0, 0, pl.ds(0, side - 1)], sh_ssem.at[l, 0])
+        wait_block(sh_all.at[l, 0, pl.ds(0, 2)], sh_ssem.at[l, 1])
+        wait_block(sh_all.at[l, 0, 0], sh_ssem.at[l, 2])
+        wait_block(sh_all.at[l, 0], sh_ssem.at[l, 3])
+
+    def turn_ahead(l, first, last):
+        if l + 1 >= layers:
+            return
+
+        def one(g, c):
+            wait_group(l + 1, g)
+            for j in range(GROUP_SEQS):
+                b = g * GROUP_SEQS + j
+                cache_v[0, b, 0:LATENT, :] = cache_v[l + 1, b, 0:LATENT, :].T
+            return c
+
+        lax.fori_loop(first, last, one, 0)
+
+    for l in range(layers):
+        if l > 0:
+            spread_2(l)
         x = x_s[...]
         hidden = rms_norm(x).astype(BF16)
         q = dot32(hidden, wq_v[l]).astype(BF16).astype(F32)
@@ -220,7 +242,18 @@
             return e * (1.0 / jnp.sum(e, axis=-1, keepdims=True))
 
         def value_step(acc, p, g, j):
-            return jnp.where(row8v == j, dot_nt(p, cache_v[l, g * GROUP_SEQS + j, 0:LATENT, :]), acc)
+            if l > 0:
+                o = dot32(p, cache_v[0, g * GROUP_SEQS + j, 0:LATENT, :])
+            elif j < TURNED:
+                o = dot32(p, turn_s[g % 2 if isinstance(g, int) else lax.rem(g, 2), j])
+            else:
+                o = dot_nt(p, cache_v[l, g * GROUP_SEQS + j, 0:LATENT, :])
+            return jnp.where(row8v == j, o, acc)
+
+        def turn_step(g, j):
+            if l == 0 and j < TURNED:
+                slot = g % 2 if isinstance(g, int) else lax.rem(g, 2)
+                turn_s[slot, j] = cache_v[l, g * GROUP_SEQS + j, 0:LATENT, :].T
 
         def put_out(acc, g):
             og = acc
@@ -231,32 +264,40 @@
         no_score = jnp.full((2 * GROUP_SEQS, seq_len), -jnp.inf, F32)
         no_out = jnp.zeros((2 * GROUP_SEQS, LATENT), F32)
 
-        wait_group(l, 0)
         s = no_score
         qg = q_s[0].astype(BF16)
         for j in range(GROUP_SEQS):
+            if l == 0 and j % HALF == 0:
+                wait_half(l, j // HALF)
             s = score_step(s, qg, 0, j)
+            turn_step(0, j)
         p_s[...] = softmax(s)
 
-        @pl.when(l == 0)
-        def _():
+        if l == 0:
             pl.semaphore_wait(barrier, group - 1)
-
-        spread_1(l)
+            spread_1(l)
 
         def attend(g, c):
-            wait_group(l, g + 1)
+            if l == 0:
+                wait_group(l, g + 1)
             p = p_s[...].astype(BF16)
             qg = q_s[g + 1].astype(BF16)
             s, acc = no_score, no_out
             for j in range(GROUP_SEQS):
                 s = score_step(s, qg, g + 1, j)
                 acc = value_step(acc, p, g, j)
+                turn_step(g + 1, j)
             p_s[...] = softmax(s)
             put_out(acc, g)
             @pl.when(g == n_groups // 2 - 1)
             def _():
-                spread_2(l)
+                if l == 0:
+                    spread_2(l)
+
+            if l + 1 < layers:
+                @pl.when(g == n_groups - 2)
+                def _():
+                    start_halves(l + 1, 0, n_halves)
             return c
 
         lax.fori_loop(0, n_groups - 1, attend, 0)
@@ -266,8 +307,7 @@
             acc = value_step(acc, p, n_groups - 1, j)
         put_out(acc, n_groups - 1)
 
-        @pl.when(l == 0)
-        def _():
+        if l == 0:
             for name in ('wo', 'w1e', 'w3e', 'w2e', 'wq1', 'rw'):
                 copies[name].wait()
 
@@ -280,18 +320,10 @@
             remote(d_send.at[l, :, dev, used], d_recv.at[l, :, me, used], d_ssem.at[0], d_rsem.at[0], dev).start()
         d_recv[l, :, me] = d_send[l, :, me]
         spread_3(l)
-
-        @pl.when(l + 1 < layers)
-        def _():
-            start_layer(l + 1)
-
-        @pl.when(l == 0)
-        def _():
-            for other in range(1, layers):
-                build_dispatch(other)
-            for other in range(layers):
-                build_select(other)
-
+        build_select(l)
+        if l + 1 < layers:
+            build_dispatch(l + 1)
+        turn_ahead(l, 0, n_groups // 2)
         wait_all_peers(d_recv.at[l], d_rsem.at[0])
         spread_4(l)
         for n in range(local_experts):
@@ -305,6 +337,8 @@
             remote(r_send.at[l, :, dev, used], r_recv.at[l, :, me, used], r_ssem.at[0], r_rsem.at[0], dev).start()
         r_recv[l, :, me] = r_send[l, :, me]
         spread_end(l)
+        if l + 1 < layers:
+            spread_1(l + 1)
         hid = group * SHARD_ROWS
         ffn_in = rms_norm(x1_s[...]).astype(BF16)
         up = dot_nt(ffn_in, sh_all[l, :, :, :, 0].reshape(hid, d_model))
@@ -312,6 +346,7 @@
         sh_h = (silu(gate) * up).astype(BF16)
         x1_s[...] = x1_s[...] + dot32(sh_h, sh_all[l, :, :, :, 2].reshape(hid, d_model))
         wait_all_peers(d_send.at[l], d_ssem.at[0])
+        turn_ahead(l, n_groups // 2, n_groups)
         wait_all_peers(r_recv.at[l], r_rsem.at[0])
         picked = dot32(sel_s[l], r_recv[l].reshape(n_rows, d_model))
         rw = rwt_s[l]
@@ -320,9 +355,6 @@
             routed = routed + rw[:, j:j + 1] * picked[j * batch:(j + 1) * batch]
         x_s[...] = (x1_s[...] + routed).astype(BF16).astype(F32)
         wait_all_peers(r_send.at[l], r_ssem.at[0])
-        return carry
-
-    lax.fori_loop(0, layers, layer, 0)
     out_ref[...] = x_s[...].astype(BF16)
 
 
@@ -347,7 +379,7 @@
         top_k = expert_ids.shape[2]
         n_rows = local_experts * group * SLOT_ROWS
         vmem = pl.BlockSpec(memory_space=pltpu.VMEM)
-        hbm = pl.BlockSpec(memory_space=pl.ANY)
+        hbm = pl.BlockSpec(memory_space=pltpu.HBM)
         block = (layers, local_experts, group, SLOT_ROWS, d_model)
         expert = (layers, local_experts, ff, d_model)
         route = (top_k, layers, batch)
@@ -370,6 +402,7 @@
             pltpu.VMEM((batch, 2 * LATENT), F32),
             pltpu.VMEM((batch, d_model), F32),
             pltpu.VMEM((batch, d_model), F32),
+            pltpu.VMEM((2, TURNED, seq_len, LATENT), BF16),
             pltpu.VMEM((8, 128), F32),
             pltpu.VMEM((8, 128), F32),
             pltpu.VMEM((layers, batch, 8), F32),
@@ -381,19 +414,19 @@
             pltpu.VMEM(block, BF16),
             pltpu.VMEM(block, BF16),
             pltpu.VMEM(block, BF16),
-            pltpu.SemaphoreType.DMA((layers, batch // GROUP_SEQS)),
+            pltpu.SemaphoreType.DMA((layers, batch // HALF)),
             pltpu.SemaphoreType.DMA((14,)),
-            pltpu.SemaphoreType.DMA((4,)),
-            pltpu.SemaphoreType.DMA((4,)),
+            pltpu.SemaphoreType.DMA((layers, 4)),
+            pltpu.SemaphoreType.DMA((layers, 4)),
             one_sem, one_sem, one_sem, one_sem,
         ]
         return pl.pallas_call(
             functools.partial(step_kernel, group, side),
-            out_shape=jax.ShapeDtypeStruct((batch, d_model), BF16),
+            out_shape=pltpu.VMEM((batch, d_model), BF16),
             in_specs=[hbm] * 14,
             out_specs=vmem,
             scratch_shapes=scratch,
-            compiler_params=pltpu.CompilerParams(collective_id=0, has_side_effects=True, vmem_limit_bytes=60 * 1024 * 1024),
+            compiler_params=pltpu.CompilerParams(collective_id=0, has_side_effects=True, vmem_limit_bytes=56 * 1024 * 1024),
         )(
             lengths, x, jnp.swapaxes(cache, 2, 3), w_q, w_o,
             jnp.transpose(expert_ids, (2, 0, 1)), jnp.transpose(slots, (2, 0, 1)), jnp.transpose(route_w, (2, 0, 1)),

time: 50.8 us -> 46.4 us (0.913)
  Pallas kernels: 49.3 us -> 45.7 us
  local copies, waits for them, and re-layouts: 1.32 us -> 0.61 us
    pallas_call x1, Pallas kernels: 49.3 us -> 45.7 us  [device_step(): pl.pallas_call(functools.partial(step_kernel, group, side), out_shape=plt...]
    unnamed x1, local copies, waits for them, and re-layouts: 1.32 us -> 0.61 us
where the time goes in v3:
time: 46.4 us; the launch traced here: 46.3 us
  Pallas kernels  45.7 us (98%)
  local copies, waits for them, and re-layouts  0.61 us (1%)
    pallas_call x1, Pallas kernels, device_step(): pl.pallas_call(functools.partial(step_kernel, group, side), out_shape=plt...  45.7 us

profile of v3, /device:TPU:97, one launch (start us, length us, event | category | flops | bytes accessed | tf_op | source)
XLA Modules:
  0.0 46.3 jit_solution(4621064494746251825)
XLA Ops:
  0.0 45.7 %shard_map.136 = bf16[32,256]{1,0:T(8,128)(2,1)S(1)} custom-call(s32[32]{0:T(128)} %lengths.1, bf16[32,256]{1,0:T(8,128)(2,1)} %x_in.1, bf16[2,32,576,512]{3,2,1,0:T(8,128)(2,1)} %bitcast.9, bf16[2,256,1152]{2,1,0:T(8,128)(2,1)} %w_q.1, bf16[2,1024,256]{2,1,0:T(8,128)(2,1)} %w_o.1, s32[6,2,32]{2,1,0:T(2,128)} %bitcast.15, s32[6,2,32]{2,1,0:T(2,128)} %bitcast.16, ...), custom_call_target="tpu_custom_call" | custom-call | tf_op jit(solution)/shard_map/pallas_call | solution.py:423
  45.7 0.6 %copy.16 = bf16[32,256]{1,0:T(8,128)(2,1)} copy(bf16[32,256]{1,0:T(8,128)(2,1)S(1)} %shard_map.136) | data formatting | bytes 32768

commit v4 on v3

--- a/solution.py
+++ b/solution.py
@@ -12,7 +12,9 @@
 LATENT = 512
 GROUP_SEQS = 8
 HALF = 4
-TURNED = 5
+TURNED = 7
+TURNED_HALF = 4
+SPREAD2_AT = 2
 SLOT_ROWS = 8
 SHARD_ROWS = 16
 F32 = jnp.float32
@@ -222,90 +224,80 @@
 
         lax.fori_loop(first, last, one, 0)
 
+    whole = [(b, GROUP_SEQS) for b in range(0, batch, GROUP_SEQS)]
+    inner = [(b, GROUP_SEQS) for b in range(HALF, batch - HALF, GROUP_SEQS)]
+    segments = [[(0, HALF)] + inner + [(batch - HALF, HALF)]] + [whole] * (layers - 1)
+
     for l in range(layers):
         if l > 0:
             spread_2(l)
-        x = x_s[...]
-        hidden = rms_norm(x).astype(BF16)
+        segs = segments[l]
+        hidden = rms_norm(x_s[...]).astype(BF16)
         q = dot32(hidden, wq_v[l]).astype(BF16).astype(F32)
-        for g in range(n_groups):
-            for h in range(2):
-                q_s[g, h * GROUP_SEQS:(h + 1) * GROUP_SEQS, :] = q[g * GROUP_SEQS:(g + 1) * GROUP_SEQS, h * kv_dim:(h + 1) * kv_dim]
-
-        def score_step(s, qg, g, j):
-            sj = dot32(qg, cache_v[l, g * GROUP_SEQS + j]) * ATT_SCALE
-            keep = jnp.logical_and(row8 == j, t_iota < len_s[g * GROUP_SEQS + j])
+        for k, (start, count) in enumerate(segs):
+            for b in range(start, start + count, HALF):
+                for h in range(2):
+                    row = h * GROUP_SEQS + b % GROUP_SEQS
+                    q_s[k, row:row + HALF, :] = q[b:b + HALF, h * kv_dim:(h + 1) * kv_dim]
+
+        def turned(k, b):
+            return l == 0 and b - segs[k][0] < (TURNED if segs[k][1] == GROUP_SEQS else TURNED_HALF)
+
+        def score_step(s, qg, k, b):
+            sj = dot32(qg, cache_v[l, b]) * ATT_SCALE
+            keep = jnp.logical_and(row8 == b % GROUP_SEQS, t_iota < len_s[b])
+            if turned(k, b):
+                turn_s[k % 2, b - segs[k][0]] = cache_v[l, b, 0:LATENT, :].T
             return jnp.where(keep, sj, s)
+
+        def value_step(acc, p, k, b):
+            if l > 0:
+                o = dot32(p, cache_v[0, b, 0:LATENT, :])
+            elif turned(k, b):
+                o = dot32(p, turn_s[k % 2, b - segs[k][0]])
+            else:
+                o = dot_nt(p, cache_v[l, b, 0:LATENT, :])
+            return jnp.where(row8v == b % GROUP_SEQS, o, acc)
 
         def softmax(s):
             e = jnp.exp(s - jnp.max(s, axis=-1, keepdims=True))
             return e * (1.0 / jnp.sum(e, axis=-1, keepdims=True))
 
-        def value_step(acc, p, g, j):
-            if l > 0:
-                o = dot32(p, cache_v[0, g * GROUP_SEQS + j, 0:LATENT, :])
-            elif j < TURNED:
-                o = dot32(p, turn_s[g % 2 if isinstance(g, int) else lax.rem(g, 2), j])
-            else:
-                o = dot_nt(p, cache_v[l, g * GROUP_SEQS + j, 0:LATENT, :])
-            return jnp.where(row8v == j, o, acc)
-
-        def turn_step(g, j):
-            if l == 0 and j < TURNED:
-                slot = g % 2 if isinstance(g, int) else lax.rem(g, 2)
-                turn_s[slot, j] = cache_v[l, g * GROUP_SEQS + j, 0:LATENT, :].T
-
-        def put_out(acc, g):
-            og = acc
-            rows_g = pl.ds(pl.multiple_of(g * GROUP_SEQS, GROUP_SEQS), GROUP_SEQS)
-            o_s[rows_g, 0:LATENT] = og[0:GROUP_SEQS]
-            o_s[rows_g, LATENT:2 * LATENT] = og[GROUP_SEQS:2 * GROUP_SEQS]
-
-        no_score = jnp.full((2 * GROUP_SEQS, seq_len), -jnp.inf, F32)
-        no_out = jnp.zeros((2 * GROUP_SEQS, LATENT), F32)
-
-        s = no_score
-        qg = q_s[0].astype(BF16)
-        for j in range(GROUP_SEQS):
-            if l == 0 and j % HALF == 0:
-                wait_half(l, j // HALF)
-            s = score_step(s, qg, 0, j)
-            turn_step(0, j)
-        p_s[...] = softmax(s)
-
-        if l == 0:
-            pl.semaphore_wait(barrier, group - 1)
-            spread_1(l)
-
-        def attend(g, c):
-            if l == 0:
-                wait_group(l, g + 1)
-            p = p_s[...].astype(BF16)
-            qg = q_s[g + 1].astype(BF16)
-            s, acc = no_score, no_out
+        def attend(before, k):
+            s, acc, p, qg = None, None, None, None
+            steps = []
+            if k is not None:
+                if l == 0:
+                    for b in range(segs[k][0], sum(segs[k]), HALF) if k < last else ():
+                        wait_half(l, b // HALF)
+                s, qg = jnp.full((2 * GROUP_SEQS, seq_len), -jnp.inf, F32), q_s[k].astype(BF16)
+            if before is not None:
+                acc, p = jnp.zeros((2 * GROUP_SEQS, LATENT), F32), p_s[...].astype(BF16)
             for j in range(GROUP_SEQS):
-                s = score_step(s, qg, g + 1, j)
-                acc = value_step(acc, p, g, j)
-                turn_step(g + 1, j)
-            p_s[...] = softmax(s)
-            put_out(acc, g)
-            @pl.when(g == n_groups // 2 - 1)
-            def _():
-                if l == 0:
-                    spread_2(l)
-
-            if l + 1 < layers:
-                @pl.when(g == n_groups - 2)
-                def _():
-                    start_halves(l + 1, 0, n_halves)
-            return c
-
-        lax.fori_loop(0, n_groups - 1, attend, 0)
-        p = p_s[...].astype(BF16)
-        acc = no_out
-        for j in range(GROUP_SEQS):
-            acc = value_step(acc, p, n_groups - 1, j)
-        put_out(acc, n_groups - 1)
+                if k is not None and j < segs[k][1]:
+                    s = score_step(s, qg, k, segs[k][0] + j)
+                if before is not None and j < segs[before][1]:
+                    acc = value_step(acc, p, before, segs[before][0] + j)
+            if k is not None:
+                p_s[...] = softmax(s)
+            if before is not None:
+                for b in range(segs[before][0], sum(segs[before]), HALF):
+                    for h in range(2):
+                        row = h * GROUP_SEQS + b % GROUP_SEQS
+                        o_s[b:b + HALF, h * LATENT:(h + 1) * LATENT] = acc[row:row + HALF]
+
+        last = len(segs) - 1
+        for k in range(len(segs) + 1):
+            if l + 1 < layers and k == last:
+                for b in range(segs[k][0], sum(segs[k]), HALF):
+                    wait_half(l, b // HALF)
+                start_halves(l + 1, 0, n_halves)
+            attend(k - 1 if k > 0 else None, k if k <= last else None)
+            if l == 0 and k == 0:
+                pl.semaphore_wait(barrier, group - 1)
+                spread_1(l)
+            if l == 0 and k == SPREAD2_AT:
+                spread_2(l)
 
         if l == 0:
             for name in ('wo', 'w1e', 'w3e', 'w2e', 'wq1', 'rw'):
@@ -397,7 +389,7 @@
             pltpu.VMEM(expert, BF16),
             pltpu.VMEM(expert, BF16),
             pltpu.VMEM(expert, BF16),
-            pltpu.VMEM((batch // GROUP_SEQS, 2 * GROUP_SEQS, kv_dim), F32),
+            pltpu.VMEM((batch // GROUP_SEQS + 1, 2 * GROUP_SEQS, kv_dim), F32),
             pltpu.VMEM((2 * GROUP_SEQS, seq_len), F32),
             pltpu.VMEM((batch, 2 * LATENT), F32),
             pltpu.VMEM((batch, d_model), F32),

time: 46.4 us -> 45.6 us (0.983)
  Pallas kernels: 45.7 us -> 44.9 us
    pallas_call x1, Pallas kernels: 45.7 us -> 44.9 us  [device_step(): pl.pallas_call(functools.partial(step_kernel, group, side), out_shape=plt...]
where the time goes in v4:
time: 45.6 us
  Pallas kernels  44.9 us (98%)
  local copies, waits for them, and re-layouts  0.61 us (1%)
    pallas_call x1, Pallas kernels, device_step(): pl.pallas_call(functools.partial(step_kernel, group, side), out_shape=plt...  44.9 us

profile of v4, /device:TPU:97, one launch (start us, length us, event | category | flops | bytes accessed | tf_op | source)
XLA Modules:
  0.0 45.6 jit_solution(10412172724557026523)
XLA Ops:
  0.0 44.9 %shard_map.136 = bf16[32,256]{1,0:T(8,128)(2,1)S(1)} custom-call(s32[32]{0:T(128)} %lengths.1, bf16[32,256]{1,0:T(8,128)(2,1)} %x_in.1, bf16[2,32,576,512]{3,2,1,0:T(8,128)(2,1)} %bitcast.9, bf16[2,256,1152]{2,1,0:T(8,128)(2,1)} %w_q.1, bf16[2,1024,256]{2,1,0:T(8,128)(2,1)} %w_o.1, s32[6,2,32]{2,1,0:T(2,128)} %bitcast.15, s32[6,2,32]{2,1,0:T(2,128)} %bitcast.16, ...), custom_call_target="tpu_custom_call" | custom-call | tf_op jit(solution)/shard_map/pallas_call | solution.py:415
  45.0 0.6 %copy.16 = bf16[32,256]{1,0:T(8,128)(2,1)} copy(bf16[32,256]{1,0:T(8,128)(2,1)S(1)} %shard_map.136) | data formatting | bytes 32768

commit v5 on v4

--- a/solution.py
+++ b/solution.py
@@ -86,10 +86,13 @@
         ))
     }
 
+    def cache_slot(l, k):
+        return k if l == 0 else batch // HALF + k // 2
+
     def start_half(l, k):
         def one(j, c):
             b = k * HALF + j
-            pltpu.make_async_copy(cache.at[l, b], cache_v.at[l, b], cache_sem.at[l, k]).start()
+            pltpu.make_async_copy(cache.at[l, b], cache_v.at[l, b], cache_sem.at[cache_slot(l, k)]).start()
             return c
         lax.fori_loop(0, HALF, one, 0, unroll=True)
 
@@ -101,11 +104,11 @@
 
     def wait_half(l, k):
         rows = pl.ds(k * HALF, HALF)
-        pltpu.make_async_copy(cache.at[l, rows], cache_v.at[l, rows], cache_sem.at[l, k]).wait()
+        pltpu.make_async_copy(cache.at[l, rows], cache_v.at[l, rows], cache_sem.at[cache_slot(l, k)]).wait()
 
     def wait_group(l, g):
-        wait_half(l, 2 * g)
-        wait_half(l, 2 * g + 1)
+        rows = pl.ds(g * GROUP_SEQS, GROUP_SEQS)
+        pltpu.make_async_copy(cache.at[l, rows], cache_v.at[l, rows], cache_sem.at[cache_slot(l, 2 * g)]).wait()
 
     n_halves = batch // HALF
     for name in ('x', 's0', 's1', 's2', 'ids', 'slots', 'len', 'wq0'):
@@ -183,33 +186,33 @@
         sh_all[l, core, row_a, col_b] = sh_send[l]
         for k in (2, 1, 3):
             dev = device_at(row_a, lax.rem(col_b + k, side))
-            remote(sh_send.at[l], sh_all.at[l, core, row_a, col_b], sh_ssem.at[l, 0], sh_rsem.at[l, 0], dev).start()
+            remote(sh_send.at[l], sh_all.at[l, core, row_a, col_b], sh_ssem.at[0], sh_rsem.at[0], dev).start()
 
     def spread_2(l):
-        wait_block(sh_all.at[l, 0, 0, pl.ds(0, side - 1)], sh_rsem.at[l, 0])
+        wait_block(sh_all.at[l, 0, 0, pl.ds(0, side - 1)], sh_rsem.at[0])
         line = sh_all.at[l, core, row_a]
         for k in (1, side - 1):
             dev = device_at(lax.rem(row_a + k, side), col_b)
-            remote(line, line, sh_ssem.at[l, 1], sh_rsem.at[l, 1], dev).start()
+            remote(line, line, sh_ssem.at[1], sh_rsem.at[1], dev).start()
 
     def spread_3(l):
-        wait_block(sh_all.at[l, 0, pl.ds(0, 2)], sh_rsem.at[l, 1])
+        wait_block(sh_all.at[l, 0, pl.ds(0, 2)], sh_rsem.at[1])
         for k, half in ((1, 0), (side - 1, side // 2)):
             dev = device_at(lax.rem(row_a + k, side), col_b)
             part = sh_all.at[l, core, lax.rem(row_a + side - k, side), pl.ds(half, side // 2)]
-            remote(part, part, sh_ssem.at[l, 2], sh_rsem.at[l, 2], dev).start()
+            remote(part, part, sh_ssem.at[2], sh_rsem.at[2], dev).start()
 
     def spread_4(l):
-        wait_block(sh_all.at[l, 0, 0], sh_rsem.at[l, 2])
+        wait_block(sh_all.at[l, 0, 0], sh_rsem.at[2])
         half = sh_all.at[l, core]
-        remote(half, half, sh_ssem.at[l, 3], sh_rsem.at[l, 3], me + 1 - 2 * core).start()
+        remote(half, half, sh_ssem.at[3], sh_rsem.at[3], me + 1 - 2 * core).start()
 
     def spread_end(l):
-        wait_block(sh_all.at[l, 0], sh_rsem.at[l, 3])
-        wait_block(sh_all.at[l, 0, 0, pl.ds(0, side - 1)], sh_ssem.at[l, 0])
-        wait_block(sh_all.at[l, 0, pl.ds(0, 2)], sh_ssem.at[l, 1])
-        wait_block(sh_all.at[l, 0, 0], sh_ssem.at[l, 2])
-        wait_block(sh_all.at[l, 0], sh_ssem.at[l, 3])
+        wait_block(sh_all.at[l, 0], sh_rsem.at[3])
+        wait_block(sh_all.at[l, 0, 0, pl.ds(0, side - 1)], sh_ssem.at[0])
+        wait_block(sh_all.at[l, 0, pl.ds(0, 2)], sh_ssem.at[1])
+        wait_block(sh_all.at[l, 0, 0], sh_ssem.at[2])
+        wait_block(sh_all.at[l, 0], sh_ssem.at[3])
 
     def turn_ahead(l, first, last):
         if l + 1 >= layers:
@@ -406,10 +409,10 @@
             pltpu.VMEM(block, BF16),
             pltpu.VMEM(block, BF16),
             pltpu.VMEM(block, BF16),
-            pltpu.SemaphoreType.DMA((layers, batch // HALF)),
+            pltpu.SemaphoreType.DMA((batch // HALF + batch // GROUP_SEQS,)),
             pltpu.SemaphoreType.DMA((14,)),
-            pltpu.SemaphoreType.DMA((layers, 4)),
-            pltpu.SemaphoreType.DMA((layers, 4)),
+            pltpu.SemaphoreType.DMA((4,)),
+            pltpu.SemaphoreType.DMA((4,)),
             one_sem, one_sem, one_sem, one_sem,
         ]
         return pl.pallas_call(

time: 45.6 us -> 45.6 us (level)
  no operation moved by 1% of the time
where the time goes in v5:
time: 45.6 us
  Pallas kernels  44.9 us (98%)
  local copies, waits for them, and re-layouts  0.61 us (1%)
    pallas_call x1, Pallas kernels, device_step(): pl.pallas_call(functools.partial(step_kernel, group, side), out_shape=plt...  44.9 us

profile of v5, /device:TPU:97, one launch (start us, length us, event | category | flops | bytes accessed | tf_op | source)
XLA Modules:
  0.0 45.6 jit_solution(16982793760435677444)
XLA Ops:
  0.0 44.9 %shard_map.136 = bf16[32,256]{1,0:T(8,128)(2,1)S(1)} custom-call(s32[32]{0:T(128)} %lengths.1, bf16[32,256]{1,0:T(8,128)(2,1)} %x_in.1, bf16[2,32,576,512]{3,2,1,0:T(8,128)(2,1)} %bitcast.9, bf16[2,256,1152]{2,1,0:T(8,128)(2,1)} %w_q.1, bf16[2,1024,256]{2,1,0:T(8,128)(2,1)} %w_o.1, s32[6,2,32]{2,1,0:T(2,128)} %bitcast.15, s32[6,2,32]{2,1,0:T(2,128)} %bitcast.16, ...), custom_call_target="tpu_custom_call" | custom-call | tf_op jit(solution)/shard_map/pallas_call | solution.py:418
  44.9 0.6 %copy.16 = bf16[32,256]{1,0:T(8,128)(2,1)} copy(bf16[32,256]{1,0:T(8,128)(2,1)S(1)} %shard_map.136) | data formatting | bytes 32768
